TPU v7x, 128 devices: a whole 4x4x4 slice. The times are simulated.
128 devices in a mesh: seq: 32 (over y, x, core), tp: 4 (over z).
Axes of the slice: x: 4, y: 4, z: 4, core: 2. Of those that a mesh axis runs over, the one named last changes fastest.
Arguments:
- hidden: bfloat16 [32768, 2560], P('seq', 'tp'), may hold values from -6 to 6
- gate_proj: bfloat16 [2560, 5120], P(None, 'tp'), may hold values from -0.125 to 0.125
- input_proj: bfloat16 [2560, 5120], P(None, 'tp'), may hold values from -0.125 to 0.125
- bc_proj: bfloat16 [2560, 256], replicated, may hold values from -0.125 to 0.125
- step_proj: bfloat16 [2560, 80], P(None, 'tp'), may hold values from -0.125 to 0.125
- step_bias: float32 [80], P('tp'), may hold values from -16 to -3
- decay_log: float32 [80], P('tp'), may hold values from 0 to 2.78
- conv_weight: float32 [4, 5120], P(None, 'tp'), may hold values from -3 to 3
- conv_bias: float32 [5120], P('tp'), may hold values from -3 to 3
- bc_conv_weight: float32 [4, 256], replicated, may hold values from -3 to 3
- bc_conv_bias: float32 [256], replicated, may hold values from -3 to 3
- skip_gain: float32 [80], P('tp'), may hold values from 0.5 to 2
- norm_gain: float32 [5120], P('tp'), may hold values from 0.1 to 1.9
- out_proj: bfloat16 [5120, 2560], P('tp'), may hold values from -0.078125 to 0.078125
- amax_history: float32 [16], replicated, may hold values from 1.5 to 4
Outputs:
- mixed: bfloat16 [32768, 2560], P('seq', 'tp')
- new_history: float32 [16], replicated
All inputs are finite; a program needn't handle non-finite values.
Results may differ from a plain program's by a relative error of at most 0.015.
Values may be sent and summed in bfloat16 or wider, within the bound.
A program may use at most 192 MiB of HBM per device.

v0:
```python
import jax
import jax.numpy as jnp
from jax import lax
from jax.sharding import Mesh
from jax.sharding import PartitionSpec as P

BLOCK = 256
INNER = 5120
SEQ = ("seq_0", "seq_1", "seq_2")
QMAX = 448.0
EPS = 1e-05


def shifted(x, axis, by):
    size = lax.axis_size(axis)
    pairs = [(i, i + by) for i in range(size) if 0 <= i + by < size]
    return lax.ppermute(x, axis, pairs)


def nothing_yet(x, identity):
    return jax.tree.map(
        lambda part, zero: jnp.zeros_like(part) + jnp.asarray(zero, part.dtype), x, identity
    )


def entering(x, axes, combine, identity):
    before = start = nothing_yet(x, identity)
    subtotal = x
    for axis in reversed(axes):
        size, here = (lax.axis_size(axis), lax.axis_index(axis))
        pieces = jax.tree.map(
            lambda part, kind: lax.all_gather(part.astype(kind), axis),
            subtotal,
            (jnp.bfloat16, jnp.bfloat16),
        )
        inside, subtotal = (start, start)
        for k in range(size):
            passed = k < here
            subtotal = combine(
                subtotal, jax.tree.map(lambda part, own: part[k].astype(own.dtype), pieces, x)
            )
            inside = jax.tree.map(lambda new, old: jnp.where(passed, new, old), subtotal, inside)
        before = combine(inside, before)
    return before


def from_everyone(x, axis):
    size = lax.axis_size(axis)
    return lax.all_to_all(jnp.broadcast_to(x[None], (size, *x.shape)), axis, 0, 0, tiled=True)


def gathered_once(x, axis):
    leaves = jax.tree.leaves(x)
    turns = sorted(range(len(leaves)), key=lambda k: -leaves[k].size)
    width = (1, *leaves[turns[0]].shape)[-1]
    lines = [
        jnp.pad(leaves[k].reshape(-1), (0, -leaves[k].size % width)).reshape(-1, width)
        for k in turns
    ]
    both, at, found = (from_everyone(jnp.concatenate(lines), axis), 0, {})
    for k, line in zip(turns, lines):
        section = both[:, at : at + len(line)].reshape(len(both), -1)
        found[k] = section[:, : leaves[k].size].reshape(-1, *leaves[k].shape)
        at += len(line)
    numbers = iter(range(len(leaves)))
    return jax.tree.map(lambda _: found[next(numbers)], x)


def collected_alike(x, axis):
    leaves, found = (jax.tree.leaves(x), {})
    for first, a in enumerate(leaves):
        if first not in found:
            alike = [k for k, b in enumerate(leaves) if b.dtype == a.dtype]
            got = (
                gathered_once([leaves[k] for k in alike], axis)
                if len(alike) > 1
                else [from_everyone(a, axis)]
            )
            for k, b in zip(alike, got):
                found[k] = b
    numbers = iter(range(len(leaves)))
    return jax.tree.map(lambda _: found[next(numbers)], x)


def combined_pairwise(pieces, combine):
    while len(jax.tree.leaves(pieces)[0]) > 1:
        pieces = jax.vmap(combine)(
            *(jax.tree.map(lambda part: part[side::2], pieces) for side in (0, 1))
        )
    return jax.tree.map(lambda part: part[0], pieces)


def combined_all(x, axis, combine):
    pieces = collected_alike(x, axis)
    return combined_pairwise(pieces, combine)


def of_everyone(x, axis):
    everything = from_everyone(x, axis)
    return jnp.max(everything, axis=0)


def conv_silu(pre_conv, rim_rows, weight, conv_shift):
    row_count = pre_conv.shape[0]
    kernel = weight.shape[0]
    padded = jnp.concatenate([rim_rows, pre_conv], axis=0)
    running = jnp.zeros(pre_conv.shape, jnp.float32)
    for offset in range(kernel):
        running = running + weight[offset] * padded[offset : offset + row_count].astype(jnp.float32)
    return jax.nn.silu(running + conv_shift).astype(jnp.bfloat16)


def ssd_block(carry_state, block_data):
    x_block, b_block, c_block, step_block, decay_block = block_data
    length = x_block.shape[0]
    head_count = carry_state.shape[0]
    head_width = carry_state.shape[1]
    cum_decay = jnp.cumsum(decay_block, axis=1)
    scores = jnp.dot(c_block, b_block.T, preferred_element_type=jnp.float32)
    causal = lax.broadcasted_iota(jnp.int32, (length, length), 0) >= lax.broadcasted_iota(
        jnp.int32, (length, length), 1
    )
    decay_gap = cum_decay[:, :, None] - cum_decay[:, None, :]
    decay_mask = jnp.where(causal, jnp.exp(jnp.where(causal, decay_gap, 0.0)), 0.0)
    weights = (scores[None] * decay_mask * step_block[:, None, :]).astype(jnp.bfloat16)
    x_heads = x_block.reshape(length, head_count, head_width)
    intra_out = jnp.einsum("hts,shp->htp", weights, x_heads, preferred_element_type=jnp.float32)
    inter_out = jnp.exp(cum_decay)[:, :, None] * jnp.einsum(
        "tn,hpn->htp", c_block.astype(jnp.float32), carry_state
    )
    tail_decay = jnp.exp(cum_decay[:, -1:] - cum_decay) * step_block
    x_weighted = (tail_decay.T[:, :, None] * x_heads.astype(jnp.float32)).astype(jnp.bfloat16)
    update = jnp.einsum("shp,sn->hpn", x_weighted, b_block, preferred_element_type=jnp.float32)
    next_state = jnp.exp(cum_decay[:, -1])[:, None, None] * carry_state + update
    block_out = (intra_out + inter_out).transpose(1, 0, 2).reshape(length, head_count * head_width)
    return (next_state, block_out)


def chain(earlier, later):
    return (earlier[0] + later[0], jnp.exp(later[0])[..., None, None] * earlier[1] + later[1])


def joint(first, second):
    return (first[0] + second[0], jnp.maximum(first[1], second[1]))


def shards(
    hidden,
    gate_proj,
    input_proj,
    bc_proj,
    step_proj,
    step_bias,
    decay_log,
    conv_weight,
    conv_bias,
    bc_conv_weight,
    bc_conv_bias,
    skip_gain,
    norm_gain,
    out_proj,
    amax_history,
):
    row_count = hidden.shape[0]
    inner_local = gate_proj.shape[1]
    state_width = bc_proj.shape[1] // 2
    head_count = step_proj.shape[1]
    head_width = inner_local // head_count
    kernel = conv_weight.shape[0]
    matrices = (gate_proj, input_proj, bc_proj, step_proj)
    piece = lax.all_gather(hidden, "tp", axis=1, tiled=True)
    gate_raw, x_raw, bc_raw, step_raw = tuple(
        (jnp.dot(piece, matrix, preferred_element_type=jnp.float32) for matrix in matrices)
    )
    gate_in = gate_raw.astype(jnp.bfloat16)
    x_pre = x_raw.astype(jnp.bfloat16)
    bc_pre = bc_raw.astype(jnp.bfloat16)
    x_rim, bc_rim = shifted(
        (x_pre[row_count - kernel + 1 :], bc_pre[row_count - kernel + 1 :]), SEQ, 1
    )
    x_conv = conv_silu(x_pre, x_rim, conv_weight, conv_bias)
    bc_conv = conv_silu(bc_pre, bc_rim, bc_conv_weight, bc_conv_bias)
    b_in = bc_conv[:, :state_width]
    c_out = bc_conv[:, state_width:]
    step_size = jax.nn.softplus(step_raw + step_bias)
    log_decay = step_size * -jnp.exp(decay_log)
    blocks = row_count // BLOCK
    stacked = (
        x_conv.reshape(blocks, BLOCK, inner_local),
        b_in.reshape(blocks, BLOCK, state_width),
        c_out.reshape(blocks, BLOCK, state_width),
        step_size.reshape(blocks, BLOCK, head_count).transpose(0, 2, 1),
        log_decay.reshape(blocks, BLOCK, head_count).transpose(0, 2, 1),
    )
    zero_state = jnp.zeros((head_count, head_width, state_width), jnp.float32)
    local_state, block_outs = lax.scan(ssd_block, zero_state, stacked)
    total_decay = jnp.sum(log_decay, axis=0)
    entry_decay, incoming = entering(
        (total_decay, local_state), SEQ, chain, (jnp.zeros_like(total_decay), zero_state)
    )
    reach = jnp.exp(jnp.cumsum(log_decay, axis=0))
    carried = jnp.einsum("tn,hpn->thp", c_out.astype(jnp.float32), incoming)
    ssm_out = block_outs.reshape(row_count, inner_local) + (reach[:, :, None] * carried).reshape(
        row_count, inner_local
    )
    x_heads = x_conv.reshape(row_count, head_count, head_width).astype(jnp.float32)
    ssm_out = ssm_out + (skip_gain[:, None] * x_heads).reshape(row_count, inner_local)
    gated = ssm_out * jax.nn.silu(gate_in.astype(jnp.float32))
    local_squares = jnp.sum(gated * gated, axis=1)
    row_peak = jnp.max(jnp.abs(gated * norm_gain), axis=1)
    squares, row_top = combined_all((local_squares, row_peak), "tp", joint)
    inv_rms = lax.rsqrt(squares / INNER + EPS)
    normed = gated * inv_rms[:, None] * norm_gain
    peak_value = of_everyone(jnp.max(row_top * inv_rms), SEQ)
    scale = QMAX / jnp.max(amax_history)
    quant = jnp.clip(normed * scale, -QMAX, QMAX).astype(jnp.bfloat16)
    partial_value = jnp.dot(quant, out_proj, preferred_element_type=jnp.float32)
    summed = lax.psum_scatter(
        partial_value.astype(jnp.bfloat16), "tp", scatter_dimension=1, tiled=True
    ).astype(jnp.float32)
    mixed = (summed / scale).astype(jnp.bfloat16)
    new_history = jnp.concatenate([jnp.reshape(peak_value, (1,)), amax_history[:-1]])
    return (mixed, new_history)


def solution(mesh):
    finer = Mesh(mesh.devices.reshape(4, 4, 2, mesh.shape["tp"]), ("seq_0", "seq_1", "seq_2", "tp"))
    in_specs = (
        P(SEQ, "tp"),
        P(None, "tp"),
        P(None, "tp"),
        P(),
        P(None, "tp"),
        P("tp"),
        P("tp"),
        P(None, "tp"),
        P("tp"),
        P(),
        P(),
        P("tp"),
        P("tp"),
        P("tp", None),
        P(),
    )
    out_specs = (P(SEQ, "tp"), P())
    return jax.shard_map(
        shards, mesh=finer, in_specs=in_specs, out_specs=out_specs, check_vma=False
    )
```

profile of v0, /device:TPU:1, one launch (start us, length us, event | category | flops | bytes accessed | tf_op | source)
XLA Modules:
  0.0 332.2 jit_solution(15634064660990956811)
XLA Ops:
  12.3 57.5 %all-gather.8.cloned.1.call-done = bf16[1024,2560]{1,0:T(8,128)(2,1)} async-done(((bf16[1024,640]{1,0:T(8,128)(2,1)}), bf16[1024,2560]{1,0:T(8,128)(2,1)}) %all-gather.8.cloned.1.call-update) | async-done | bytes 5242896 | tf_op jit(solution)/shard_map/all_gather | solution.py:171
  69.9 4.1 %convolution_convert_fusion.3 = bf16[1024,256]{1,0:T(8,128)(2,1)S(1)} fusion(bf16[1024,2560]{1,0:T(8,128)(2,1)} %all-gather.8.cloned.1.call-done, bf16[2560,256]{1,0:T(8,128)(2,1)S(1)} %copy-done), kind=kOutput, calls=%fused_computation.68 | convolution fusion | flops 1342439424 | bytes 7077888 | tf_op jit(solution)/shard_map/dot_general | solution.py:173
  74.1 4.0 %collective-permute-start.1 = (bf16[3,256]{1,0:T(4,128)(2,1)S(1)}, bf16[3,256]{1,0:T(4,128)(2,1)S(1)}, u32[]{:S(2)}, u32[]{:S(2)}) collective-permute-start(bf16[3,256]{1,0:T(4,128)(2,1)S(1)} %slice.240), channel_id=1, source_target_pairs={{0,4},{4,8},{8,12},{12,16},{16,20},{20,24},{24,28},{28,32},{32,36}... | collective-permute-start | bytes 4616 | tf_op jit(solution)/shard_map/ppermute | solution.py:17
  78.1 10.0 %convolution_convert_fusion.2 = bf16[1024,1280]{1,0:T(8,128)(2,1)S(1)} fusion(bf16[1024,2560]{1,0:T(8,128)(2,1)S(1)} %copy-done.3, bf16[2560,1280]{1,0:T(8,128)(2,1)} %param.19), kind=kOutput, calls=%fused_computation.55 | convolution fusion | flops 6712197120 | bytes 14417920 | tf_op jit(solution)/shard_map/dot_general | solution.py:173
  88.1 2.1 collective-permute-start
  90.2 2.2 fusion.111
  92.9 2.6 all-reduce
  97.6 8.2 %multiply_convert_fusion.4 = bf16[1024,1280]{1,0:T(8,128)(2,1)} fusion(bf16[1024,1280]{1,0:T(8,128)(2,1)} %copy-done.6, bf16[3,1280]{1,0:T(4,128)(2,1)S(1)} %collective-permute-done, f32[1280]{0:T(1024)S(1)} %copy-done.11, f32[1280]{0:T(1024)S(1)} %get-tuple-element.126, f32[1280]{0:T(1024)S(1)} %get-tuple-element.127, f32[1280]{0:T(1024)S(1)} %get-tuple-element.125, ...), kind=kLoop, calls=%fused_computation.53 | loop fusion | flops 34078720 | bytes 5276160 | tf_op jit(solution)/shard_map/convert_element_type | solution.py:110
  105.9 47.1 %while.13 = (s32[]{:T(128)}, f32[20,64,128]{2,1,0:T(8,128)S(1)}, f32[4,256,1280]{2,1,0:T(8,128)}, f32[4,20,256]{2,1,0:T(8,128)}, f32[4,20,256]{2,1,0:T(8,128)}, ...) while((s32[]{:T(128)}, f32[20,64,128]{2,1,0:T(8,128)S(1)}, ...), condition=%wide.region_3.4_spmd.clone, body=%wide.region_0.3_spmd.clone.sunk | while | flops 363210816 | bytes 22548344 | solution.py:196
  107.8 1.4 multiply_bitcast_fusion.3
  110.8 1.7 fusion.172
  119.6 1.4 multiply_bitcast_fusion.3
  122.6 1.7 fusion.172
  134.4 1.7 fusion.172
  146.2 1.7 fusion.172
  153.1 2.6 all-gather.1
  156.8 7.9 %all-gather.2 = bf16[4,1,20]{2,1,0:T(2,128)(2,1)S(1)} all-gather(bf16[1,1,20]{2,1,0:T(2,128)(2,1)} %get-tuple-element.170), channel_id=1, replica_groups=mesh['seq_0'=4,'seq_1'=4,'seq_2'=2,'tp'=4] {'seq_1'}, dimensions={0}, use_global_device_ids=true | all-gather | bytes 200 | tf_op jit(solution)/shard_map/all_gather | solution.py:32
  164.8 15.5 %all-gather.10.cloned.1.call-done = bf16[4,20,64,128]{3,2,1,0:T(8,128)(2,1)} async-done(((bf16[1,20,64,128]{3,2,1,0:T(8,128)(2,1)}), bf16[4,20,64,128]{3,2,1,0:T(8,128)(2,1)}) %all-gather.10.cloned.1.call-update) | async-done | bytes 1310736 | tf_op jit(solution)/shard_map/all_gather | solution.py:32
  180.3 2.4 fusion.60
  182.9 5.6 %reduce-window.16 = f32[20,8,128]{2,1,0:T(8,128)S(1)} reduce-window(f32[20,8,128]{2,1,0:T(8,128)S(1)} %slice.273, f32[]{:T(128)} %constant.37.clone.1), window={size=1x1x128 pad=0_0x0_0x127_0}, to_apply=%region_4.5 | reduce-window | flops 2600960 | bytes 163844 | tf_op jit(solution)/shard_map/reduce-window.2
  189.0 7.7 %all-gather.3 = bf16[4,1,20]{2,1,0:T(2,128)(2,1)S(1)} all-gather(bf16[1,1,20]{2,1,0:T(2,128)(2,1)S(1)} %get-tuple-element.164), channel_id=1, replica_groups=mesh['seq_0'=4,'seq_1'=4,'seq_2'=2,'tp'=4] {'seq_0'}, dimensions={0}, use_global_device_ids=true | all-gather | bytes 200 | tf_op jit(solution)/shard_map/all_gather | solution.py:32
  196.7 11.5 %all-gather.12.cloned.1.call-done = bf16[4,20,64,128]{3,2,1,0:T(8,128)(2,1)} async-done(((bf16[1,20,64,128]{3,2,1,0:T(8,128)(2,1)}), bf16[4,20,64,128]{3,2,1,0:T(8,128)(2,1)}) %all-gather.12.cloned.1.call-update) | async-done | bytes 1310736 | tf_op jit(solution)/shard_map/all_gather | solution.py:32
  208.3 5.8 %broadcast_multiply_fusion = f32[1024,20,64]{0,2,1:T(8,128)} fusion(f32[1024,20]{0,1:T(8,128)S(1)} %bitcast.302, bf16[4,20,64,128]{3,2,1,0:T(8,128)(2,1)} %all-gather.12.cloned.1.call-done, f32[20]{0:T(128)S(1)} %get-tuple-element.171, f32[20]{0:T(128)S(1)} %get-tuple-element.169, f32[20]{0:T(128)S(1)} %get-tuple-element.168, ...), kind=kOutput, calls=%fused_computation.66 | convolution fusion | flops 343572480 | bytes 8886282 | tf_op jit(solution)/shard_map/tn,hpn->thp/dot_general | solution.py:202
  214.1 5.9 %copy.71 = f32[1024,1280]{1,0:T(8,128)} copy(f32[1024,1280]{0,1:T(8,128)} %bitcast.291) | data formatting | bytes 10485760 | tf_op jit(solution)/shard_map/reshape | solution.py:203
  220.0 16.0 %multiply_reduce_fusion = (f32[1024]{0:T(1024)S(1)}, f32[1024]{0:T(1024)S(1)}, f32[1024,1280]{1,0:T(8,128)}) fusion(f32[1280]{0:T(1024)S(1)} %copy-done.15, bf16[1024,2560]{1,0:T(8,128)(2,1)} %all-gather.8.cloned.1.call-done, bf16[2560,1280]{1,0:T(8,128)(2,1)} %param.18, bf16[1024,1280]{1,0:T(8,128)(2,1)} %bitcast.290, f32[1280]{0:T(1024)S(1)} %mul.413, ...), kind=kOutput, calls=%fused_computation.52 | convolution fusion | flops 6731855872 | bytes 30164992 | tf_op jit(solution)/shard_map/dot_general | solution.py:173
  236.6 4.1 %all-to-all-start = ((f32[4,2,1024]{2,1,0:T(2,128)}), f32[4,2,1024]{2,1,0:T(2,128)S(1)}, u32[]{:S(2)}, u32[]{:S(2)}) async-start(f32[4,2,1024]{2,1,0:T(2,128)} %broadcast_in_dim.33), calls=%async_computation | async-start | bytes 65536 | tf_op jit(solution)/shard_map/all_to_all | solution.py:49
  242.1 3.0 all-to-all-done
  245.2 12.7 %convolution_convert_fusion = bf16[1024,2560]{1,0:T(8,128)(2,1)} fusion(bf16[1280,2560]{1,0:T(8,128)(2,1)} %param.30, f32[1024,1280]{1,0:T(8,128)} %get-tuple-element.174, f32[]{:T(128)S(6)} %div.31, f32[1024]{0:T(1024)S(1)} %bitcast.307, f32[1280]{0:T(1024)S(1)} %copy-done.15), kind=kOutput, calls=%fused_computation.43 | convolution fusion | flops 6720061440 | bytes 17048580 | tf_op jit(solution)/shard_map/dot_general | solution.py:217
  257.9 7.9 %copy.73 = bf16[1024,2560]{0,1:T(8,128)(2,1)} copy(bf16[1024,2560]{1,0:T(8,128)(2,1)} %convolution_convert_fusion) | data formatting | bytes 10485760
  267.3 16.1 %all_to_all.11 = f32[32,1,1]{2,1,0:T(1,128)S(1)} all-to-all(f32[32,1,1]{2,1,0:T(1,128)S(1)} %broadcast_in_dim.34), channel_id=1, replica_groups=mesh['seq_0'=4,'seq_1'=4,'seq_2'=2,'tp'=4] {'seq_0','seq_1','seq_2'}, dimensions={0} | all-to-all | bytes 256 | tf_op jit(solution)/shard_map/all_to_all | solution.py:49
  285.2 37.5 %reduce-scatter.4.cloned.1.call-done = bf16[640,1024]{1,0:T(8,128)(2,1)} async-done(((bf16[2560,1024]{1,0:T(8,128)(2,1)}), bf16[640,1024]{1,0:T(8,128)(2,1)}) %reduce-scatter.4.cloned.1.call-update) | async-done | bytes 1310736
  322.7 1.7 copy.74
  (206 shorter events, 51.9 us)
Async XLA Ops:
  7.2 62.7 %copy-start = (bf16[2560,256]{1,0:T(8,128)(2,1)S(1)}, bf16[2560,256]{1,0:T(8,128)(2,1)}, u32[]{:S(2)}) copy-start(bf16[2560,256]{1,0:T(8,128)(2,1)} %param.20) | copy-start | bytes 3932164
  7.2 62.7 %all-gather.8.cloned.1.call-start = ((), (), s32[]{:S(2)}) async-start(), calls=%async_computation.3 | async-start | bytes 6553600 | tf_op jit(solution)/shard_map/all_gather | solution.py:171
  7.9 172.3 %all-gather.10.cloned.1.call-start = ((), (), s32[]{:S(2)}) async-start(), calls=%async_computation.4 | async-start | bytes 1638400 | tf_op jit(solution)/shard_map/all_gather | solution.py:32
  69.9 8.2 %copy-start.3 = (bf16[1024,2560]{1,0:T(8,128)(2,1)S(1)}, bf16[1024,2560]{1,0:T(8,128)(2,1)}, u32[]{:S(2)}) copy-start(bf16[1024,2560]{1,0:T(8,128)(2,1)} %all-gather.8.cloned.1.call-done) | copy-start | bytes 15728644
  74.1 16.1 %copy-start.10 = (bf16[2560,20]{0,1:T(8,128)(2,1)S(1)}, bf16[2560,20]{0,1:T(8,128)(2,1)}, u32[]{:S(2)}) copy-start(bf16[2560,20]{0,1:T(8,128)(2,1)} %param.21) | copy-start | bytes 307204
  74.1 16.1 %copy-start.12 = (f32[20]{0:T(128)S(1)}, f32[20]{0:T(128)}, u32[]{:S(2)}) copy-start(f32[20]{0:T(128)} %param.22) | copy-start | bytes 244
  74.1 22.7 %collective-permute-start.1 = (bf16[3,256]{1,0:T(4,128)(2,1)S(1)}, bf16[3,256]{1,0:T(4,128)(2,1)S(1)}, u32[]{:S(2)}, u32[]{:S(2)}) collective-permute-start(bf16[3,256]{1,0:T(4,128)(2,1)S(1)} %slice.240), channel_id=1, source_target_pairs={{0,4},{4,8},{8,12},{12,16},{16,20},{20,24},{24,28},{28,32},{32,36}... | collective-permute-start | bytes 4616 | tf_op jit(solution)/shard_map/ppermute | solution.py:17
  88.0 4.3 %copy-start.6 = (bf16[1024,1280]{1,0:T(8,128)(2,1)}, bf16[1024,1280]{1,0:T(8,128)(2,1)S(1)}, u32[]{:S(2)}) copy-start(bf16[1024,1280]{1,0:T(8,128)(2,1)S(1)} %convolution_convert_fusion.2) | copy-start | bytes 7864324
  88.1 8.8 %copy-start.13 = (f32[256]{0:T(256)S(1)}, f32[256]{0:T(256)}, u32[]{:S(2)}) copy-start(f32[256]{0:T(256)} %param.27) | copy-start | bytes 3076
  88.1 9.5 %copy-start.11 = (f32[1280]{0:T(1024)S(1)}, f32[1280]{0:T(1024)}, u32[]{:S(2)}) copy-start(f32[1280]{0:T(1024)} %param.25) | copy-start | bytes 15364
  88.1 9.5 %collective-permute-start = (bf16[3,1280]{1,0:T(4,128)(2,1)S(1)}, bf16[3,1280]{1,0:T(4,128)(2,1)S(1)}, u32[]{:S(2)}, u32[]{:S(2)}) collective-permute-start(bf16[3,1280]{1,0:T(4,128)(2,1)S(1)} %slice.235), channel_id=1, source_target_pairs={{0,4},{4,8},{8,12},{12,16},{16,20},{20,24},{24,28},{28,32},{32,36}... | collective-permute-start | bytes 23048 | tf_op jit(solution)/shard_map/ppermute | solution.py:17
  97.5 8.3 %copy-start.7 = (bf16[1024,256]{1,0:T(8,128)(2,1)}, bf16[1024,256]{1,0:T(8,128)(2,1)S(1)}, u32[]{:S(2)}) copy-start(bf16[1024,256]{1,0:T(8,128)(2,1)S(1)} %multiply_convert_fusion.5) | copy-start | bytes 1572868
  105.9 6.6 %copy-start.4 = (bf16[4,256,128]{2,1,0:T(8,128)(2,1)}, bf16[4,256,128]{2,1,0:T(8,128)(2,1)S(1)}, u32[]{:S(2)}) copy-start(bf16[4,256,128]{2,1,0:T(8,128)(2,1)S(1)} %get-tuple-element.260) | copy-start | bytes 786436 | tf_op jit(solution)/shard_map/while
  110.8 1.7 copy-start.2
  114.0 3.6 %copy-start.5 = (bf16[4,256,128]{2,1,0:T(8,128)(2,1)S(1)}, bf16[4,256,128]{2,1,0:T(8,128)(2,1)}, u32[]{:S(2)}) copy-start(bf16[4,256,128]{2,1,0:T(8,128)(2,1)} %copy-done.4) | copy-start | bytes 786436 | tf_op jit(solution)/shard_map/while
  117.7 6.6 %copy-start.4 = (bf16[4,256,128]{2,1,0:T(8,128)(2,1)}, bf16[4,256,128]{2,1,0:T(8,128)(2,1)S(1)}, u32[]{:S(2)}) copy-start(bf16[4,256,128]{2,1,0:T(8,128)(2,1)S(1)} %get-tuple-element.260) | copy-start | bytes 786436 | tf_op jit(solution)/shard_map/while
  122.6 1.7 copy-start.2
  125.8 3.6 %copy-start.5 = (bf16[4,256,128]{2,1,0:T(8,128)(2,1)S(1)}, bf16[4,256,128]{2,1,0:T(8,128)(2,1)}, u32[]{:S(2)}) copy-start(bf16[4,256,128]{2,1,0:T(8,128)(2,1)} %copy-done.4) | copy-start | bytes 786436 | tf_op jit(solution)/shard_map/while
  129.4 6.6 %copy-start.4 = (bf16[4,256,128]{2,1,0:T(8,128)(2,1)}, bf16[4,256,128]{2,1,0:T(8,128)(2,1)S(1)}, u32[]{:S(2)}) copy-start(bf16[4,256,128]{2,1,0:T(8,128)(2,1)S(1)} %get-tuple-element.260) | copy-start | bytes 786436 | tf_op jit(solution)/shard_map/while
  134.3 1.7 copy-start.2
  137.5 3.7 %copy-start.5 = (bf16[4,256,128]{2,1,0:T(8,128)(2,1)S(1)}, bf16[4,256,128]{2,1,0:T(8,128)(2,1)}, u32[]{:S(2)}) copy-start(bf16[4,256,128]{2,1,0:T(8,128)(2,1)} %copy-done.4) | copy-start | bytes 786436 | tf_op jit(solution)/shard_map/while
  141.3 6.6 %copy-start.4 = (bf16[4,256,128]{2,1,0:T(8,128)(2,1)}, bf16[4,256,128]{2,1,0:T(8,128)(2,1)S(1)}, u32[]{:S(2)}) copy-start(bf16[4,256,128]{2,1,0:T(8,128)(2,1)S(1)} %get-tuple-element.260) | copy-start | bytes 786436 | tf_op jit(solution)/shard_map/while
  149.4 3.6 %copy-start.5 = (bf16[4,256,128]{2,1,0:T(8,128)(2,1)S(1)}, bf16[4,256,128]{2,1,0:T(8,128)(2,1)}, u32[]{:S(2)}) copy-start(bf16[4,256,128]{2,1,0:T(8,128)(2,1)} %copy-done.4) | copy-start | bytes 786436 | tf_op jit(solution)/shard_map/while
  153.0 29.7 %copy-start.14 = (f32[20]{0:T(128)S(1)}, f32[20]{0:T(128)}, u32[]{:S(2)}) copy-start(f32[20]{0:T(128)} %param.28) | copy-start | bytes 244
  153.0 29.8 %copy-start.9 = (f32[20,1024]{1,0:T(8,128)S(1)}, f32[20,1024]{1,0:T(8,128)}, u32[]{:S(2)}) copy-start(f32[20,1024]{1,0:T(8,128)} %get-tuple-element.172) | copy-start | bytes 245764
  153.0 55.2 %copy-start.8 = (bf16[1024,256]{1,0:T(8,128)(2,1)S(1)}, bf16[1024,256]{1,0:T(8,128)(2,1)}, u32[]{:S(2)}) copy-start(bf16[1024,256]{1,0:T(8,128)(2,1)} %copy-done.7) | copy-start | bytes 1572868
  156.7 51.5 %all-gather.12.cloned.1.call-start = ((), (), s32[]{:S(2)}) async-start(), calls=%async_computation.5 | async-start | bytes 1638400 | tf_op jit(solution)/shard_map/all_gather | solution.py:32
  214.1 5.9 %copy-start.15 = (f32[1280]{0:T(1024)S(1)}, f32[1280]{0:T(1024)}, u32[]{:S(2)}) copy-start(f32[1280]{0:T(1024)} %param.29) | copy-start | bytes 15364
  220.0 20.8 %copy-start.16 = (f32[16]{0:T(128)S(1)}, f32[16]{0:T(128)}, u32[]{:S(2)}) copy-start(f32[16]{0:T(128)} %param.31) | copy-start | bytes 196
  236.6 8.4 %all-to-all-start = ((f32[4,2,1024]{2,1,0:T(2,128)}), f32[4,2,1024]{2,1,0:T(2,128)S(1)}, u32[]{:S(2)}, u32[]{:S(2)}) async-start(f32[4,2,1024]{2,1,0:T(2,128)} %broadcast_in_dim.33), calls=%async_computation | async-start | bytes 65536 | tf_op jit(solution)/shard_map/all_to_all | solution.py:49
  240.8 81.9 %reduce-scatter.4.cloned.1.call-start = ((), (), s32[]{:S(2)}) async-start(), calls=%async_computation.6 | async-start | bytes 6553600
  265.9 59.8 %copy-start.1 = (bf16[2560,256]{1,0:T(8,128)(2,1)S(1)}, bf16[2560,256]{1,0:T(8,128)(2,1)}, u32[]{:S(2)}) copy-start(bf16[2560,256]{1,0:T(8,128)(2,1)} %param.20) | copy-start | bytes 3932164
  (1 other events, 1.7 us)
Sparse Core Ops, SparseCore 0:
  9.7 60.1 all-gather.7
  156.8 23.3 all-gather.9
  182.8 25.4 all-gather.11
  266.0 56.6 reduce-scatter.3
where the time goes:
time: 334 us; the launch traced here: 332 us
  waiting for transfers between devices  126 us (38%)
  matrix products  67.3 us (20%)
  local copies, waits for them, and re-layouts  38.3 us (11%)
  other arithmetic  37.7 us (11%)
  blocking collectives  36.9 us (11%)
  between operations  15.5 us (5%)
  starting transfers between devices  10.3 us (3%)
    all_gather x1, waiting for transfers between devices, shards(): piece = lax.all_gather(hidden, 'tp', axis=1, tiled=True)  57.5 us
    unnamed x5, waiting for transfers between devices  38.2 us
    dot_general x4, matrix products, shards(): jnp.dot(piece, matrix, preferred_element_type=jnp.float32)  32.3 us
    all_gather x2, waiting for transfers between devices, entering(): lax.all_gather(part.astype(kind), axis)  27 us
    all_gather x3, blocking collectives, entering(): lax.all_gather(part.astype(kind), axis)  18.2 us
    all_to_all x1, blocking collectives, from_everyone(): lax.all_to_all(jnp.broadcast_to(x[None], (size, *x.shape)), axis, 0, 0, t...  16.1 us
    dot_general x1, matrix products, shards(): partial_value = jnp.dot(quant, out_proj, preferred_element_type=jnp.float32)  12.7 us
    unnamed x38, local copies, waits for them, and re-layouts  11.3 us
  transfers between devices with their start and end apart: 7, of which 5 were waited for; matrix products, arithmetic and copies ran while one was open for 9% of the time, Pallas kernels for 0%

commit v1 on v0

--- a/solution.py
+++ b/solution.py
@@ -168,7 +168,9 @@
     head_width = inner_local // head_count
     kernel = conv_weight.shape[0]
     matrices = (gate_proj, input_proj, bc_proj, step_proj)
-    piece = lax.all_gather(hidden, "tp", axis=1, tiled=True)
+    piece = jnp.concatenate(
+        lax.all_to_all(jnp.stack([hidden] * lax.axis_size("tp")), "tp", 0, 0), axis=1
+    )
     gate_raw, x_raw, bc_raw, step_raw = tuple(
         (jnp.dot(piece, matrix, preferred_element_type=jnp.float32) for matrix in matrices)
     )

time: 334 us -> 347 us (1.039)
  starting transfers between devices: 10.3 us -> 16.7 us
  local copies, waits for them, and re-layouts: 38.3 us -> 42.2 us
    all_to_all x0 -> x1, waiting for transfers between devices: none -> 59.2 us  [shards(): lax.all_to_all(jnp.stack([hidden] * lax.axis_size('tp')), 'tp', 0, 0)]
    all_gather x1 -> x0, waiting for transfers between devices: 57.5 us -> none  [shards(): piece = lax.all_gather(hidden, 'tp', axis=1, tiled=True)]
    all_to_all x0 -> x1, starting transfers between devices: none -> 5.99 us  [shards(): lax.all_to_all(jnp.stack([hidden] * lax.axis_size('tp')), 'tp', 0, 0)]
    unnamed x38 -> x45, local copies, waits for them, and re-layouts: 11.3 us -> 13.8 us
    unnamed x5 -> x4, waiting for transfers between devices: 38.2 us -> 37.5 us
  transfers between devices with their start and end apart: 7 -> 7, of which waited for: 5 -> 5; matrix products, arithmetic and copies ran while one was open for 9% -> 8% of each run, Pallas kernels for 0% -> 0%
where the time goes in v1:
time: 347 us; the launch traced here: 345 us
  waiting for transfers between devices  125 us (36%)
  matrix products  70.6 us (20%)
  local copies, waits for them, and re-layouts  42.2 us (12%)
  blocking collectives  37.1 us (11%)
  other arithmetic  37 us (11%)
  starting transfers between devices  16.7 us (5%)
  between operations  15.5 us (4%)
    all_to_all x1, waiting for transfers between devices, shards(): lax.all_to_all(jnp.stack([hidden] * lax.axis_size('tp')), 'tp', 0, 0)  59.2 us
    unnamed x4, waiting for transfers between devices  37.5 us
    dot_general x4, matrix products, shards(): jnp.dot(piece, matrix, preferred_element_type=jnp.float32)  35.6 us
    all_gather x2, waiting for transfers between devices, entering(): lax.all_gather(part.astype(kind), axis)  25.6 us
    all_gather x3, blocking collectives, entering(): lax.all_gather(part.astype(kind), axis)  18.3 us
    all_to_all x1, blocking collectives, from_everyone(): lax.all_to_all(jnp.broadcast_to(x[None], (size, *x.shape)), axis, 0, 0, t...  16.1 us
    unnamed x45, local copies, waits for them, and re-layouts  13.8 us
    dot_general x1, matrix products, shards(): partial_value = jnp.dot(quant, out_proj, preferred_element_type=jnp.float32)  12.7 us
  transfers between devices with their start and end apart: 7, of which 5 were waited for; matrix products, arithmetic and copies ran while one was open for 8% of the time, Pallas kernels for 0%

profile of v1, /device:TPU:1, one launch (start us, length us, event | category | flops | bytes accessed | tf_op | source)
XLA Modules:
  0.0 345.1 jit_solution(67153863533296586)
XLA Ops:
  7.2 1.7 copy.69
  8.9 3.1 stack.2
  12.0 6.0 %all-to-all-start = ((bf16[4,1024,640]{1,2,0:T(8,128)(2,1)}), bf16[4,1024,640]{1,2,0:T(8,128)(2,1)}, u32[]{:S(2)}, u32[]{:S(2)}) async-start(bf16[4,1024,640]{1,2,0:T(8,128)(2,1)} %stack.2), calls=%async_computation | async-start | bytes 10485760 | tf_op jit(solution)/shard_map/all_to_all | solution.py:172
  19.3 59.2 %all-to-all-done = bf16[4,1024,640]{1,2,0:T(8,128)(2,1)} async-done(((bf16[4,1024,640]{1,2,0:T(8,128)(2,1)}), bf16[4,1024,640]{1,2,0:T(8,128)(2,1)}, u32[]{:S(2)}, u32[]{:S(2)}) %all-to-all-start) | async-done | bytes 5242912 | tf_op jit(solution)/shard_map/all_to_all | solution.py:172
  78.5 4.1 %convolution_convert_fusion.3 = bf16[1024,256]{1,0:T(8,128)(2,1)S(1)} fusion(bf16[1024,2560]{0,1:T(8,128)(2,1)} %bitcast.1, bf16[2560,256]{1,0:T(8,128)(2,1)S(1)} %copy-done), kind=kOutput, calls=%fused_computation.68 | convolution fusion | flops 1342439424 | bytes 7077888 | tf_op jit(solution)/shard_map/dot_general | solution.py:175
  82.6 4.5 %collective-permute-start.1 = (bf16[3,256]{1,0:T(4,128)(2,1)S(1)}, bf16[3,256]{1,0:T(4,128)(2,1)S(1)}, u32[]{:S(2)}, u32[]{:S(2)}) collective-permute-start(bf16[3,256]{1,0:T(4,128)(2,1)S(1)} %slice.240), channel_id=1, source_target_pairs={{0,4},{4,8},{8,12},{12,16},{16,20},{20,24},{24,28},{28,32},{32,36}... | collective-permute-start | bytes 4616 | tf_op jit(solution)/shard_map/ppermute | solution.py:17
  87.1 10.9 %convolution_convert_fusion.2 = bf16[1024,1280]{1,0:T(8,128)(2,1)S(1)} fusion(bf16[1024,2560]{0,1:T(8,128)(2,1)} %bitcast.1, bf16[2560,1280]{1,0:T(8,128)(2,1)} %param.19), kind=kOutput, calls=%fused_computation.55 | convolution fusion | flops 6712197120 | bytes 14417920 | tf_op jit(solution)/shard_map/dot_general | solution.py:175
  99.6 2.1 collective-permute-start
  101.6 4.0 %fusion.111 = (f32[20,1024]{1,0:T(8,128)}, f32[1024,20]{0,1:T(8,128)S(1)}) fusion(f32[20]{0:T(128)S(1)} %exponential_negate_fusion, f32[20]{0:T(128)S(1)} %copy-done.12, bf16[1024,2560]{0,1:T(8,128)(2,1)} %bitcast.1, bf16[2560,20]{0,1:T(8,128)(2,1)S(1)} %copy-done.9), kind=kOutput, calls=%fused_computation.161 | convolution fusion | flops 105021440 | bytes 5509280 | tf_op jit(solution)/shard_map/dot_general | solution.py:175
  106.1 2.8 all-reduce
  111.1 8.2 %multiply_convert_fusion.4 = bf16[1024,1280]{1,0:T(8,128)(2,1)} fusion(bf16[1024,1280]{1,0:T(8,128)(2,1)} %copy-done.5, bf16[3,1280]{1,0:T(4,128)(2,1)S(1)} %collective-permute-done, f32[1280]{0:T(1024)S(1)} %copy-done.11, f32[1280]{0:T(1024)S(1)} %get-tuple-element.126, f32[1280]{0:T(1024)S(1)} %get-tuple-element.127, f32[1280]{0:T(1024)S(1)} %get-tuple-element.125, ...), kind=kLoop, calls=%fused_computation.53 | loop fusion | flops 34078720 | bytes 5276160 | tf_op jit(solution)/shard_map/convert_element_type | solution.py:110
  119.3 47.1 %while.13 = (s32[]{:T(128)}, f32[20,64,128]{2,1,0:T(8,128)S(1)}, f32[4,256,1280]{2,1,0:T(8,128)}, f32[4,20,256]{2,1,0:T(8,128)}, f32[4,20,256]{2,1,0:T(8,128)}, ...) while((s32[]{:T(128)}, f32[20,64,128]{2,1,0:T(8,128)S(1)}, ...), condition=%wide.region_3.4_spmd.clone, body=%wide.region_0.3_spmd.clone.sunk | while | flops 363210816 | bytes 22548344 | solution.py:198
  124.3 1.7 fusion.172
  136.1 1.7 fusion.172
  147.8 1.7 fusion.172
  166.5 2.4 all-gather.1
  170.1 8.0 %all-gather.2 = bf16[4,1,20]{2,1,0:T(2,128)(2,1)S(1)} all-gather(bf16[1,1,20]{2,1,0:T(2,128)(2,1)} %get-tuple-element.170), channel_id=1, replica_groups=mesh['seq_0'=4,'seq_1'=4,'seq_2'=2,'tp'=4] {'seq_1'}, dimensions={0}, use_global_device_ids=true | all-gather | bytes 200 | tf_op jit(solution)/shard_map/all_gather | solution.py:32
  178.1 14.3 %all-gather.7.cloned.1.call-done = bf16[4,20,64,128]{3,2,1,0:T(8,128)(2,1)} async-done(((bf16[1,20,64,128]{3,2,1,0:T(8,128)(2,1)}), bf16[4,20,64,128]{3,2,1,0:T(8,128)(2,1)}) %all-gather.7.cloned.1.call-update) | async-done | bytes 1310736 | tf_op jit(solution)/shard_map/all_gather | solution.py:32
  192.4 2.4 fusion.60
  195.0 5.6 %reduce-window.16 = f32[20,8,128]{2,1,0:T(8,128)S(1)} reduce-window(f32[20,8,128]{2,1,0:T(8,128)S(1)} %slice.273, f32[]{:T(128)} %constant.37.clone.1), window={size=1x1x128 pad=0_0x0_0x127_0}, to_apply=%region_4.5 | reduce-window | flops 2600960 | bytes 163844 | tf_op jit(solution)/shard_map/reduce-window.2
  201.2 7.9 %all-gather.3 = bf16[4,1,20]{2,1,0:T(2,128)(2,1)S(1)} all-gather(bf16[1,1,20]{2,1,0:T(2,128)(2,1)S(1)} %get-tuple-element.164), channel_id=1, replica_groups=mesh['seq_0'=4,'seq_1'=4,'seq_2'=2,'tp'=4] {'seq_0'}, dimensions={0}, use_global_device_ids=true | all-gather | bytes 200 | tf_op jit(solution)/shard_map/all_gather | solution.py:32
  209.1 11.3 %all-gather.9.cloned.1.call-done = bf16[4,20,64,128]{3,2,1,0:T(8,128)(2,1)} async-done(((bf16[1,20,64,128]{3,2,1,0:T(8,128)(2,1)}), bf16[4,20,64,128]{3,2,1,0:T(8,128)(2,1)}) %all-gather.9.cloned.1.call-update) | async-done | bytes 1310736 | tf_op jit(solution)/shard_map/all_gather | solution.py:32
  220.4 5.8 %broadcast_multiply_fusion = f32[1024,20,64]{0,2,1:T(8,128)} fusion(f32[1024,20]{0,1:T(8,128)S(1)} %bitcast.305, bf16[4,20,64,128]{3,2,1,0:T(8,128)(2,1)} %all-gather.9.cloned.1.call-done, f32[20]{0:T(128)S(1)} %get-tuple-element.171, f32[20]{0:T(128)S(1)} %get-tuple-element.169, f32[20]{0:T(128)S(1)} %get-tuple-element.168, f32[20]{0:T(128)S(1)} %get-tuple-element.167, ...), kind=kOutput, calls=%fused_computation.66 | convolution fusion | flops 343572480 | bytes 8886282 | tf_op jit(solution)/shard_map/tn,hpn->thp/dot_general | solution.py:204
  226.2 5.9 %copy.76 = f32[1024,1280]{1,0:T(8,128)} copy(f32[1024,1280]{0,1:T(8,128)} %bitcast.294) | data formatting | bytes 10485760 | tf_op jit(solution)/shard_map/reshape | solution.py:205
  232.1 16.7 %multiply_reduce_fusion = (f32[1024]{0:T(1024)S(1)}, f32[1024]{0:T(1024)S(1)}, f32[1024,1280]{1,0:T(8,128)}) fusion(f32[1280]{0:T(1024)S(1)} %copy-done.16, bf16[1024,2560]{0,1:T(8,128)(2,1)} %bitcast.1, bf16[2560,1280]{1,0:T(8,128)(2,1)} %param.18, bf16[1024,1280]{1,0:T(8,128)(2,1)} %bitcast.293, f32[1280]{0:T(1024)S(1)} %mul.413, f32[1024,1280]{1,0:T(8,128)} %copy.76, ...), kind=kOutput, calls=%fused_computation.52 | convolution fusion | flops 6731855872 | bytes 30164992 | tf_op jit(solution)/shard_map/dot_general | solution.py:175
  249.4 4.1 %all-to-all-start.1 = ((f32[4,2,1024]{2,1,0:T(2,128)}), f32[4,2,1024]{2,1,0:T(2,128)S(1)}, u32[]{:S(2)}, u32[]{:S(2)}) async-start(f32[4,2,1024]{2,1,0:T(2,128)} %broadcast_in_dim.33), calls=%async_computation.1 | async-start | bytes 65536 | tf_op jit(solution)/shard_map/all_to_all | solution.py:49
  254.9 3.0 all-to-all-done.1
  258.0 12.7 %convolution_convert_fusion = bf16[1024,2560]{1,0:T(8,128)(2,1)} fusion(bf16[1280,2560]{1,0:T(8,128)(2,1)} %param.30, f32[1024,1280]{1,0:T(8,128)} %get-tuple-element.174, f32[]{:T(128)S(6)} %div.31, f32[1024]{0:T(1024)S(1)} %bitcast.310, f32[1280]{0:T(1024)S(1)} %copy-done.16), kind=kOutput, calls=%fused_computation.43 | convolution fusion | flops 6720061440 | bytes 17048580 | tf_op jit(solution)/shard_map/dot_general | solution.py:219
  270.7 7.9 %copy.78 = bf16[1024,2560]{0,1:T(8,128)(2,1)} copy(bf16[1024,2560]{1,0:T(8,128)(2,1)} %convolution_convert_fusion) | data formatting | bytes 10485760
  280.1 16.1 %all_to_all.16 = f32[32,1,1]{2,1,0:T(1,128)S(1)} all-to-all(f32[32,1,1]{2,1,0:T(1,128)S(1)} %broadcast_in_dim.34), channel_id=1, replica_groups=mesh['seq_0'=4,'seq_1'=4,'seq_2'=2,'tp'=4] {'seq_0','seq_1','seq_2'}, dimensions={0} | all-to-all | bytes 256 | tf_op jit(solution)/shard_map/all_to_all | solution.py:49
  298.0 37.5 %reduce-scatter.4.cloned.1.call-done = bf16[640,1024]{1,0:T(8,128)(2,1)} async-done(((bf16[2560,1024]{1,0:T(8,128)(2,1)}), bf16[640,1024]{1,0:T(8,128)(2,1)}) %reduce-scatter.4.cloned.1.call-update) | async-done | bytes 1310736
  335.5 1.7 copy.79
  (213 shorter events, 54.1 us)
Async XLA Ops:
  7.2 71.3 %copy-start = (bf16[2560,256]{1,0:T(8,128)(2,1)S(1)}, bf16[2560,256]{1,0:T(8,128)(2,1)}, u32[]{:S(2)}) copy-start(bf16[2560,256]{1,0:T(8,128)(2,1)} %param.20) | copy-start | bytes 3932164
  12.0 6.0 %copy-start.19 = (u32[128]{0:T(128)S(1)}, u32[128]{0:T(128)}, u32[]{:S(2)}) copy-start(u32[128]{0:T(128)} %constant.71) | copy-start | bytes 1540
  12.0 7.2 %copy-start.10 = (f32[4,1280]{1,0:T(4,128)S(1)}, f32[4,1280]{1,0:T(4,128)}, u32[]{:S(2)}) copy-start(f32[4,1280]{1,0:T(4,128)} %param.24) | copy-start | bytes 61444
  12.0 7.3 %copy-start.17 = (f32[20]{0:T(128)S(1)}, f32[20]{0:T(128)}, u32[]{:S(2)}) copy-start(f32[20]{0:T(128)} %param.23) | copy-start | bytes 244
  12.0 7.3 %copy-start.13 = (f32[4,256]{1,0:T(4,128)S(1)}, f32[4,256]{1,0:T(4,128)}, u32[]{:S(2)}) copy-start(f32[4,256]{1,0:T(4,128)} %param.26) | copy-start | bytes 12292
  12.0 66.5 %all-to-all-start = ((bf16[4,1024,640]{1,2,0:T(8,128)(2,1)}), bf16[4,1024,640]{1,2,0:T(8,128)(2,1)}, u32[]{:S(2)}, u32[]{:S(2)}) async-start(bf16[4,1024,640]{1,2,0:T(8,128)(2,1)} %stack.2), calls=%async_computation | async-start | bytes 10485760 | tf_op jit(solution)/shard_map/all_to_all | solution.py:172
  18.0 174.4 %all-gather.7.cloned.1.call-start = ((), (), s32[]{:S(2)}) async-start(), calls=%async_computation.4 | async-start | bytes 1638400 | tf_op jit(solution)/shard_map/all_gather | solution.py:32
  82.6 19.1 %copy-start.9 = (bf16[2560,20]{0,1:T(8,128)(2,1)S(1)}, bf16[2560,20]{0,1:T(8,128)(2,1)}, u32[]{:S(2)}) copy-start(bf16[2560,20]{0,1:T(8,128)(2,1)} %param.21) | copy-start | bytes 307204
  82.6 19.1 %copy-start.12 = (f32[20]{0:T(128)S(1)}, f32[20]{0:T(128)}, u32[]{:S(2)}) copy-start(f32[20]{0:T(128)} %param.22) | copy-start | bytes 244
  82.6 27.7 %collective-permute-start.1 = (bf16[3,256]{1,0:T(4,128)(2,1)S(1)}, bf16[3,256]{1,0:T(4,128)(2,1)S(1)}, u32[]{:S(2)}, u32[]{:S(2)}) collective-permute-start(bf16[3,256]{1,0:T(4,128)(2,1)S(1)} %slice.240), channel_id=1, source_target_pairs={{0,4},{4,8},{8,12},{12,16},{16,20},{20,24},{24,28},{28,32},{32,36}... | collective-permute-start | bytes 4616 | tf_op jit(solution)/shard_map/ppermute | solution.py:17
  99.5 10.7 %copy-start.14 = (f32[256]{0:T(256)S(1)}, f32[256]{0:T(256)}, u32[]{:S(2)}) copy-start(f32[256]{0:T(256)} %param.27) | copy-start | bytes 3076
  99.6 11.5 %copy-start.11 = (f32[1280]{0:T(1024)S(1)}, f32[1280]{0:T(1024)}, u32[]{:S(2)}) copy-start(f32[1280]{0:T(1024)} %param.25) | copy-start | bytes 15364
  99.6 11.5 %collective-permute-start = (bf16[3,1280]{1,0:T(4,128)(2,1)S(1)}, bf16[3,1280]{1,0:T(4,128)(2,1)S(1)}, u32[]{:S(2)}, u32[]{:S(2)}) collective-permute-start(bf16[3,1280]{1,0:T(4,128)(2,1)S(1)} %slice.235), channel_id=1, source_target_pairs={{0,4},{4,8},{8,12},{12,16},{16,20},{20,24},{24,28},{28,32},{32,36}... | collective-permute-start | bytes 23048 | tf_op jit(solution)/shard_map/ppermute | solution.py:17
  111.0 8.3 %copy-start.6 = (bf16[1024,256]{1,0:T(8,128)(2,1)}, bf16[1024,256]{1,0:T(8,128)(2,1)S(1)}, u32[]{:S(2)}) copy-start(bf16[1024,256]{1,0:T(8,128)(2,1)S(1)} %multiply_convert_fusion.5) | copy-start | bytes 1572868
  119.3 6.6 %copy-start.3 = (bf16[4,256,128]{2,1,0:T(8,128)(2,1)}, bf16[4,256,128]{2,1,0:T(8,128)(2,1)S(1)}, u32[]{:S(2)}) copy-start(bf16[4,256,128]{2,1,0:T(8,128)(2,1)S(1)} %get-tuple-element.260) | copy-start | bytes 786436 | tf_op jit(solution)/shard_map/while
  124.2 1.7 copy-start.2
  127.4 3.6 %copy-start.4 = (bf16[4,256,128]{2,1,0:T(8,128)(2,1)S(1)}, bf16[4,256,128]{2,1,0:T(8,128)(2,1)}, u32[]{:S(2)}) copy-start(bf16[4,256,128]{2,1,0:T(8,128)(2,1)} %copy-done.3) | copy-start | bytes 786436 | tf_op jit(solution)/shard_map/while
  131.1 6.6 %copy-start.3 = (bf16[4,256,128]{2,1,0:T(8,128)(2,1)}, bf16[4,256,128]{2,1,0:T(8,128)(2,1)S(1)}, u32[]{:S(2)}) copy-start(bf16[4,256,128]{2,1,0:T(8,128)(2,1)S(1)} %get-tuple-element.260) | copy-start | bytes 786436 | tf_op jit(solution)/shard_map/while
  139.2 3.6 %copy-start.4 = (bf16[4,256,128]{2,1,0:T(8,128)(2,1)S(1)}, bf16[4,256,128]{2,1,0:T(8,128)(2,1)}, u32[]{:S(2)}) copy-start(bf16[4,256,128]{2,1,0:T(8,128)(2,1)} %copy-done.3) | copy-start | bytes 786436 | tf_op jit(solution)/shard_map/while
  142.8 6.6 %copy-start.3 = (bf16[4,256,128]{2,1,0:T(8,128)(2,1)}, bf16[4,256,128]{2,1,0:T(8,128)(2,1)S(1)}, u32[]{:S(2)}) copy-start(bf16[4,256,128]{2,1,0:T(8,128)(2,1)S(1)} %get-tuple-element.260) | copy-start | bytes 786436 | tf_op jit(solution)/shard_map/while
  151.0 3.7 %copy-start.4 = (bf16[4,256,128]{2,1,0:T(8,128)(2,1)S(1)}, bf16[4,256,128]{2,1,0:T(8,128)(2,1)}, u32[]{:S(2)}) copy-start(bf16[4,256,128]{2,1,0:T(8,128)(2,1)} %copy-done.3) | copy-start | bytes 786436 | tf_op jit(solution)/shard_map/while
  154.7 6.6 %copy-start.3 = (bf16[4,256,128]{2,1,0:T(8,128)(2,1)}, bf16[4,256,128]{2,1,0:T(8,128)(2,1)S(1)}, u32[]{:S(2)}) copy-start(bf16[4,256,128]{2,1,0:T(8,128)(2,1)S(1)} %get-tuple-element.260) | copy-start | bytes 786436 | tf_op jit(solution)/shard_map/while
  162.8 3.6 %copy-start.4 = (bf16[4,256,128]{2,1,0:T(8,128)(2,1)S(1)}, bf16[4,256,128]{2,1,0:T(8,128)(2,1)}, u32[]{:S(2)}) copy-start(bf16[4,256,128]{2,1,0:T(8,128)(2,1)} %copy-done.3) | copy-start | bytes 786436 | tf_op jit(solution)/shard_map/while
  166.5 28.4 %copy-start.15 = (f32[20]{0:T(128)S(1)}, f32[20]{0:T(128)}, u32[]{:S(2)}) copy-start(f32[20]{0:T(128)} %param.28) | copy-start | bytes 244
  166.5 28.5 %copy-start.8 = (f32[20,1024]{1,0:T(8,128)S(1)}, f32[20,1024]{1,0:T(8,128)}, u32[]{:S(2)}) copy-start(f32[20,1024]{1,0:T(8,128)} %get-tuple-element.172) | copy-start | bytes 245764
  166.5 53.9 %copy-start.7 = (bf16[1024,256]{1,0:T(8,128)(2,1)S(1)}, bf16[1024,256]{1,0:T(8,128)(2,1)}, u32[]{:S(2)}) copy-start(bf16[1024,256]{1,0:T(8,128)(2,1)} %copy-done.6) | copy-start | bytes 1572868
  170.0 50.4 %all-gather.9.cloned.1.call-start = ((), (), s32[]{:S(2)}) async-start(), calls=%async_computation.5 | async-start | bytes 1638400 | tf_op jit(solution)/shard_map/all_gather | solution.py:32
  226.2 5.9 %copy-start.16 = (f32[1280]{0:T(1024)S(1)}, f32[1280]{0:T(1024)}, u32[]{:S(2)}) copy-start(f32[1280]{0:T(1024)} %param.29) | copy-start | bytes 15364
  232.1 21.5 %copy-start.18 = (f32[16]{0:T(128)S(1)}, f32[16]{0:T(128)}, u32[]{:S(2)}) copy-start(f32[16]{0:T(128)} %param.31) | copy-start | bytes 196
  249.4 8.4 %all-to-all-start.1 = ((f32[4,2,1024]{2,1,0:T(2,128)}), f32[4,2,1024]{2,1,0:T(2,128)S(1)}, u32[]{:S(2)}, u32[]{:S(2)}) async-start(f32[4,2,1024]{2,1,0:T(2,128)} %broadcast_in_dim.33), calls=%async_computation.1 | async-start | bytes 65536 | tf_op jit(solution)/shard_map/all_to_all | solution.py:49
  253.6 81.9 %reduce-scatter.4.cloned.1.call-start = ((), (), s32[]{:S(2)}) async-start(), calls=%async_computation.6 | async-start | bytes 6553600
  278.7 59.9 %copy-start.1 = (bf16[2560,256]{1,0:T(8,128)(2,1)S(1)}, bf16[2560,256]{1,0:T(8,128)(2,1)}, u32[]{:S(2)}) copy-start(bf16[2560,256]{1,0:T(8,128)(2,1)} %param.20) | copy-start | bytes 3932164
  (4 other events, 6.7 us)
Sparse Core Ops, SparseCore 0:
  170.1 22.2 all-gather.6
  194.9 25.4 all-gather.8
  278.8 56.6 reduce-scatter.3
